TPU v7x, 32 devices: a whole 2x2x4 slice. The times are simulated.
32 devices in a mesh: band: 8 (over z, x), space: 4 (over y, core).
Axes of the slice: x: 2, y: 2, z: 4, core: 2. Of those that a mesh axis runs over, the one named last changes fastest.
Arguments:
- orbitals: bfloat16 [64, 64, 160, 128], P('band', None, 'space'), may hold values from -8.5 to 8.5
- occupations: float32 [64], P('band'), may hold values from 0.07 to 2.5
Outputs:
- potential: float32 [64, 160, 128], P('band', 'space')
All inputs are finite; a program needn't handle non-finite values.
Results may differ from a plain program's by a relative error of at most 0.0003.
Values sent between devices are 32-bit elements; how exact they have to be, the bound alone decides.
A program may use at most 64 MiB of HBM per device.

v0:
```python
import math
import jax
import jax.numpy as jnp
from jax import lax
from jax.sharding import PartitionSpec as P

ITERS = 3
four_pi = 4.0 * math.pi


def with_halo(shard, sides, width):
    for axis, dim in sides:
        peers, length = (lax.axis_size(axis), shard.shape[dim])
        up = [(i, (i + 1) % peers) for i in range(peers - 1)]
        down = [(j, i) for i, j in up]
        last = lax.slice_in_dim(shard, length - width, length, axis=dim)
        first = lax.slice_in_dim(shard, 0, width, axis=dim)
        before = lax.ppermute(last, axis, up)
        after = lax.ppermute(first, axis, down)
        shard = jnp.concatenate([before, shard, after], axis=dim)
    return shard


def stencil(padded):
    center = padded[2:-2, 2:-2, 2:-2]
    near = padded[3:-1, 2:-2, 2:-2] + padded[1:-3, 2:-2, 2:-2]
    near = near + padded[2:-2, 3:-1, 2:-2] + padded[2:-2, 1:-3, 2:-2]
    near = near + padded[2:-2, 2:-2, 3:-1] + padded[2:-2, 2:-2, 1:-3]
    distant = padded[4:, 2:-2, 2:-2] + padded[:-4, 2:-2, 2:-2]
    distant = distant + padded[2:-2, 4:, 2:-2] + padded[2:-2, :-4, 2:-2]
    distant = distant + padded[2:-2, 2:-2, 4:] + padded[2:-2, 2:-2, :-4]
    return 7.5 * center - 4.0 / 3.0 * near + 1.0 / 12.0 * distant


def operate(field):
    widened = with_halo(field, (("band", 0), ("space", 1)), 2)
    return stencil(jnp.pad(widened, ((0, 0), (0, 0), (2, 2))))


def paired_sums(residual, image):
    return lax.psum((jnp.sum(residual * residual), jnp.sum(residual * image)), ("band", "space"))


def local(orbitals, occupations):

    def accumulate(index, total):
        wave = lax.dynamic_index_in_dim(orbitals, index, 0, keepdims=False).astype(jnp.float32)
        return total + occupations[index] * wave * wave

    start = jnp.zeros(orbitals.shape[1:], jnp.float32)
    partial_value = lax.fori_loop(0, orbitals.shape[0], accumulate, start)
    groups = lax.axis_size("band")
    summed = lax.psum(partial_value, "band")
    share = orbitals.shape[1] // groups
    mine = lax.dynamic_slice_in_dim(summed, lax.axis_index("band") * share, share, 0)
    density = mine / (orbitals.shape[0] * groups)
    source = four_pi * density
    potential = jnp.zeros_like(source)
    residual = source
    image = operate(residual)
    norm_now, product = paired_sums(residual, image)
    alpha = norm_now / product
    direction, along = (residual, image)
    for step in range(ITERS):
        potential = potential + alpha * direction
        residual = residual - alpha * along
        if step + 1 < ITERS:
            image = operate(residual)
            norm_next, product = paired_sums(residual, image)
            ratio = norm_next / norm_now
            alpha = norm_next / (product - ratio * norm_next / alpha)
            direction = residual + ratio * direction
            along = image + ratio * along
            norm_now = norm_next
    return potential


def solution(mesh):
    in_specs = (P("band", None, "space", None), P("band"))
    out_specs = P("band", "space", None)
    return jax.shard_map(local, mesh=mesh, in_specs=in_specs, out_specs=out_specs, check_vma=False)
```

profile of v0, /device:TPU:0, one launch (start us, length us, event | category | flops | bytes accessed | tf_op | source)
XLA Modules:
  0.0 320.6 jit_solution(14691085561565989361)
XLA Ops:
  6.5 30.2 %while.14 = (s32[]{:T(128)}, f32[64,40,128]{2,1,0:T(8,128)S(1)}, f32[8]{0:T(128)}, bf16[8,64,40,128]{3,2,1,0:T(8,128)(2,1)}, s32[]{:T(128)}, /*index=5*/s32[]{:T(128)}) while((s32[]{:T(128)}, f32[64,40,128]{2,1,0:T(8,128)S(1)}, f32[8]{0:T(128)}, bf16[8,64,40,128]{3,2,1,0:T(8,128)(2,1)}, s32[]{:T(128)}, /*index=5*/s32[]{:T(128)}) %tuple.46), condition=%wide.region_1.2_spmd.clone, body=%wide.region_0.1_spmd.clone.sunk | while | flops 1638403 | bytes 3276907 | solution.py:51
  6.5 1.3 dynamic_slice.31
  7.8 2.5 fusion.46
  10.3 1.3 dynamic_slice.31
  11.6 2.5 fusion.46
  14.1 1.3 dynamic_slice.31
  15.4 2.5 fusion.46
  17.9 1.3 dynamic_slice.31
  19.2 2.5 fusion.46
  21.6 1.3 dynamic_slice.31
  22.9 2.5 fusion.46
  25.4 1.3 dynamic_slice.31
  26.7 2.5 fusion.46
  29.2 1.3 dynamic_slice.31
  30.5 2.5 fusion.46
  33.0 1.3 dynamic_slice.31
  34.3 2.5 fusion.46
  36.8 1.1 copy-done
  37.9 86.5 %all-reduce.8.cloned.1.call-done = f32[64,40,128]{2,1,0:T(8,128)} async-done(((f32[64,40,128]{2,1,0:T(8,128)}), f32[64,40,128]{2,1,0:T(8,128)}) %all-reduce.8.cloned.1.call-update) | async-done | bytes 1310736 | tf_op jit(solution)/shard_map/psum | solution.py:53
  124.4 0.9 dynamic-slice_multiply_fusion
  125.3 3.4 %collective-permute-start.1 = (f32[2,40,128]{2,1,0:T(8,128)S(1)}, f32[2,40,128]{2,1,0:T(8,128)S(1)}, u32[]{:S(2)}, u32[]{:S(2)}) collective-permute-start(f32[2,40,128]{2,1,0:T(8,128)S(1)} %get-tuple-element.138), channel_id=1, source_target_pairs={{0,4},{4,8},{8,12},{12,16},{16,20},{20,24},{24,28},{1,5},{5,9},{9,... | collective-permute-start | bytes 122888 | tf_op jit(solution)/shard_map/ppermute | solution.py:18
  128.7 1.3 collective-permute-start
  130.0 0.4 collective-permute-done.1
  130.3 4.2 %collective-permute-done = f32[2,40,128]{2,1,0:T(8,128)S(1)} collective-permute-done((f32[2,40,128]{2,1,0:T(8,128)S(1)}, f32[2,40,128]{2,1,0:T(8,128)S(1)}, u32[]{:S(2)}, u32[]{:S(2)}) %collective-permute-start) | collective-permute-done | bytes 40992 | tf_op jit(solution)/shard_map/ppermute | solution.py:19
  134.6 1.3 collective-permute-start.3
  135.9 1.3 collective-permute-start.2
  137.2 3.5 %collective-permute-done.2 = f32[12,2,128]{2,1,0:T(2,128)S(1)} collective-permute-done((f32[12,2,128]{2,1,0:T(2,128)S(1)}, f32[12,2,128]{2,1,0:T(2,128)S(1)}, u32[]{:S(2)}, u32[]{:S(2)}) %collective-permute-start.2) | collective-permute-done | bytes 12320 | tf_op jit(solution)/shard_map/ppermute | solution.py:19
  141.0 1.8 multiply_reduce_fusion.3
  142.8 41.2 %all-reduce.5 = (f32[]{:T(128)}, f32[]{:T(128)}) all-reduce(f32[]{:T(128)} %get-tuple-element.105, f32[]{:T(128)} %get-tuple-element.104), channel_id=1, replica_groups=mesh['band'=8,'space'=4] {'band','space'}, use_global_device_ids=true, to_apply=%region_4.5 | all-reduce | flops 2 | bytes 16 | tf_op jit(solution)/shard_map/psum | solution.py:41
  185.3 0.9 multiply_subtract_fusion.1
  186.3 4.2 %collective-permute-start.5 = (f32[2,40,128]{2,1,0:T(8,128)S(1)}, f32[2,40,128]{2,1,0:T(8,128)S(1)}, u32[]{:S(2)}, u32[]{:S(2)}) collective-permute-start(f32[2,40,128]{2,1,0:T(8,128)S(1)} %get-tuple-element.136), channel_id=1, source_target_pairs={{0,4},{4,8},{8,12},{12,16},{16,20},{20,24},{24,28},{1,5},{5,9},{9,... | collective-permute-start | bytes 122888 | tf_op jit(solution)/shard_map/ppermute | solution.py:18
  190.5 1.3 collective-permute-start.4
  191.8 0.4 collective-permute-done.5
  192.1 4.2 %collective-permute-done.4 = f32[2,40,128]{2,1,0:T(8,128)S(1)} collective-permute-done((f32[2,40,128]{2,1,0:T(8,128)S(1)}, f32[2,40,128]{2,1,0:T(8,128)S(1)}, u32[]{:S(2)}, u32[]{:S(2)}) %collective-permute-start.4) | collective-permute-done | bytes 40992 | tf_op jit(solution)/shard_map/ppermute | solution.py:19
  196.4 1.3 collective-permute-start.7
  197.7 1.3 collective-permute-start.6
  199.0 2.8 collective-permute-done.6
  202.1 0.9 multiply_reduce_fusion.1
  203.0 41.9 %all-reduce.4 = (f32[]{:T(128)}, f32[]{:T(128)}) all-reduce(f32[]{:T(128)} %get-tuple-element.103, f32[]{:T(128)} %get-tuple-element.102), channel_id=1, replica_groups=mesh['band'=8,'space'=4] {'band','space'}, use_global_device_ids=true, to_apply=%region_8.9 | all-reduce | flops 2 | bytes 16 | tf_op jit(solution)/shard_map/psum | solution.py:41
  249.4 4.2 %collective-permute-start.9 = (f32[2,40,128]{2,1,0:T(8,128)S(1)}, f32[2,40,128]{2,1,0:T(8,128)S(1)}, u32[]{:S(2)}, u32[]{:S(2)}) collective-permute-start(f32[2,40,128]{2,1,0:T(8,128)S(1)} %get-tuple-element.134), channel_id=1, source_target_pairs={{0,4},{4,8},{8,12},{12,16},{16,20},{20,24},{24,28},{1,5},{5,9},{9,... | collective-permute-start | bytes 122888 | tf_op jit(solution)/shard_map/ppermute | solution.py:18
  253.6 1.3 collective-permute-start.8
  255.2 4.2 %collective-permute-done.8 = f32[2,40,128]{2,1,0:T(8,128)S(1)} collective-permute-done((f32[2,40,128]{2,1,0:T(8,128)S(1)}, f32[2,40,128]{2,1,0:T(8,128)S(1)}, u32[]{:S(2)}, u32[]{:S(2)}) %collective-permute-start.8) | collective-permute-done | bytes 40992 | tf_op jit(solution)/shard_map/ppermute | solution.py:19
  259.5 1.3 collective-permute-start.11
  260.8 1.3 collective-permute-start.10
  262.1 3.1 collective-permute-done.10
  265.6 0.9 fusion.39
  266.5 41.9 %all-reduce.3 = (f32[]{:T(128)}, f32[]{:T(128)}) all-reduce(f32[]{:T(128)} %get-tuple-element.101, f32[]{:T(128)} %get-tuple-element.100), channel_id=1, replica_groups=mesh['band'=8,'space'=4] {'band','space'}, use_global_device_ids=true, to_apply=%region_12.13 | all-reduce | flops 2 | bytes 16 | tf_op jit(solution)/shard_map/psum | solution.py:41
  312.1 1.6 multiply_add_fusion
  (21 shorter events, 1.4 us)
Async XLA Ops:
  6.5 117.8 %all-reduce.8.cloned.1.call-start = ((), (), s32[]{:S(2)}) async-start(), calls=%async_computation | async-start | bytes 2621440 | tf_op jit(solution)/shard_map/psum | solution.py:53
  36.7 1.1 copy-start
  125.3 5.0 %collective-permute-start.1 = (f32[2,40,128]{2,1,0:T(8,128)S(1)}, f32[2,40,128]{2,1,0:T(8,128)S(1)}, u32[]{:S(2)}, u32[]{:S(2)}) collective-permute-start(f32[2,40,128]{2,1,0:T(8,128)S(1)} %get-tuple-element.138), channel_id=1, source_target_pairs={{0,4},{4,8},{8,12},{12,16},{16,20},{20,24},{24,28},{1,5},{5,9},{9,... | collective-permute-start | bytes 122888 | tf_op jit(solution)/shard_map/ppermute | solution.py:18
  128.7 5.9 %collective-permute-start = (f32[2,40,128]{2,1,0:T(8,128)S(1)}, f32[2,40,128]{2,1,0:T(8,128)S(1)}, u32[]{:S(2)}, u32[]{:S(2)}) collective-permute-start(f32[2,40,128]{2,1,0:T(8,128)S(1)} %get-tuple-element.139), channel_id=1, source_target_pairs={{4,0},{8,4},{12,8},{16,12},{20,16},{24,20},{28,24},{5,1},{9,5},{13... | collective-permute-start | bytes 122888 | tf_op jit(solution)/shard_map/ppermute | solution.py:19
  134.6 2.6 collective-permute-start.3
  135.9 4.8 %collective-permute-start.2 = (f32[12,2,128]{2,1,0:T(2,128)S(1)}, f32[12,2,128]{2,1,0:T(2,128)S(1)}, u32[]{:S(2)}, u32[]{:S(2)}) collective-permute-start(f32[12,2,128]{2,1,0:T(2,128)S(1)} %get-tuple-element.133), channel_id=1, source_target_pairs={{1,0},{2,1},{3,2},{5,4},{6,5},{7,6},{9,8},{10,9},{11,10},{13,12},{... | collective-permute-start | bytes 36872 | tf_op jit(solution)/shard_map/ppermute | solution.py:19
  186.3 5.8 %collective-permute-start.5 = (f32[2,40,128]{2,1,0:T(8,128)S(1)}, f32[2,40,128]{2,1,0:T(8,128)S(1)}, u32[]{:S(2)}, u32[]{:S(2)}) collective-permute-start(f32[2,40,128]{2,1,0:T(8,128)S(1)} %get-tuple-element.136), channel_id=1, source_target_pairs={{0,4},{4,8},{8,12},{12,16},{16,20},{20,24},{24,28},{1,5},{5,9},{9,... | collective-permute-start | bytes 122888 | tf_op jit(solution)/shard_map/ppermute | solution.py:18
  190.5 5.9 %collective-permute-start.4 = (f32[2,40,128]{2,1,0:T(8,128)S(1)}, f32[2,40,128]{2,1,0:T(8,128)S(1)}, u32[]{:S(2)}, u32[]{:S(2)}) collective-permute-start(f32[2,40,128]{2,1,0:T(8,128)S(1)} %get-tuple-element.137), channel_id=1, source_target_pairs={{4,0},{8,4},{12,8},{16,12},{20,16},{24,20},{28,24},{5,1},{9,5},{13... | collective-permute-start | bytes 122888 | tf_op jit(solution)/shard_map/ppermute | solution.py:19
  196.4 2.6 collective-permute-start.7
  197.7 4.1 %collective-permute-start.6 = (f32[12,2,128]{2,1,0:T(2,128)S(1)}, f32[12,2,128]{2,1,0:T(2,128)S(1)}, u32[]{:S(2)}, u32[]{:S(2)}) collective-permute-start(f32[12,2,128]{2,1,0:T(2,128)S(1)} %get-tuple-element.129), channel_id=1, source_target_pairs={{1,0},{2,1},{3,2},{5,4},{6,5},{7,6},{9,8},{10,9},{11,10},{13,12},{... | collective-permute-start | bytes 36872 | tf_op jit(solution)/shard_map/ppermute | solution.py:19
  249.4 5.8 %collective-permute-start.9 = (f32[2,40,128]{2,1,0:T(8,128)S(1)}, f32[2,40,128]{2,1,0:T(8,128)S(1)}, u32[]{:S(2)}, u32[]{:S(2)}) collective-permute-start(f32[2,40,128]{2,1,0:T(8,128)S(1)} %get-tuple-element.134), channel_id=1, source_target_pairs={{0,4},{4,8},{8,12},{12,16},{16,20},{20,24},{24,28},{1,5},{5,9},{9,... | collective-permute-start | bytes 122888 | tf_op jit(solution)/shard_map/ppermute | solution.py:18
  253.6 5.9 %collective-permute-start.8 = (f32[2,40,128]{2,1,0:T(8,128)S(1)}, f32[2,40,128]{2,1,0:T(8,128)S(1)}, u32[]{:S(2)}, u32[]{:S(2)}) collective-permute-start(f32[2,40,128]{2,1,0:T(8,128)S(1)} %get-tuple-element.135), channel_id=1, source_target_pairs={{4,0},{8,4},{12,8},{16,12},{20,16},{24,20},{28,24},{5,1},{9,5},{13... | collective-permute-start | bytes 122888 | tf_op jit(solution)/shard_map/ppermute | solution.py:19
  259.5 2.6 collective-permute-start.11
  260.8 4.4 %collective-permute-start.10 = (f32[12,2,128]{2,1,0:T(2,128)S(1)}, f32[12,2,128]{2,1,0:T(2,128)S(1)}, u32[]{:S(2)}, u32[]{:S(2)}) collective-permute-start(f32[12,2,128]{2,1,0:T(2,128)S(1)} %get-tuple-element.125), channel_id=1, source_target_pairs={{1,0},{2,1},{3,2},{5,4},{6,5},{7,6},{9,8},{10,9},{11,10},{13,12},{... | collective-permute-start | bytes 36872 | tf_op jit(solution)/shard_map/ppermute | solution.py:19
Sparse Core Ops, SparseCore 0:
  38.0 86.3 all-reduce.7
where the time goes:
time: 322 us; the launch traced here: 321 us
  blocking collectives  125 us (39%)
  waiting for transfers between devices  110 us (34%)
  other arithmetic  27.8 us (9%)
  starting transfers between devices  23.4 us (7%)
  between operations  23 us (7%)
  local copies, waits for them, and re-layouts  11.5 us (4%)
    psum x3, blocking collectives, paired_sums(): lax.psum((jnp.sum(residual * residual), jnp.sum(residual * image)), ('ban...  125 us
    psum x1, waiting for transfers between devices, local(): summed = lax.psum(partial_value, 'band')  86.5 us
    ppermute x6, waiting for transfers between devices, with_halo(): after = lax.ppermute(first, axis, down)  22.1 us
    add x8, other arithmetic, accumulate(): return total + occupations[index] * wave * wave  19.6 us
    ppermute x6, starting transfers between devices, with_halo(): before = lax.ppermute(last, axis, up)  15.6 us
    dynamic_slice x8, local copies, waits for them, and re-layouts, accumulate(): return total + occupations[index] * wave * wave  10.4 us
    ppermute x6, starting transfers between devices, with_halo(): after = lax.ppermute(first, axis, down)  7.75 us
  transfers between devices with their start and end apart: 13, of which 10 were waited for; matrix products, arithmetic and copies ran while one was open for 0% of the time, Pallas kernels for 0%

commit v1 on v0

--- a/solution.py
+++ b/solution.py
@@ -38,7 +38,9 @@
 
 
 def paired_sums(residual, image):
-    return lax.psum((jnp.sum(residual * residual), jnp.sum(residual * image)), ("band", "space"))
+    return lax.psum(
+        lax.psum((jnp.sum(residual * residual), jnp.sum(residual * image)), "space"), "band"
+    )
 
 
 def local(orbitals, occupations):

time: 322 us -> 279 us (0.87)
  blocking collectives: 125 us -> 83.8 us
  starting transfers between devices: 23.4 us -> 19.5 us
    psum x3 -> x6, blocking collectives: 125 us -> 83.8 us  [the longest x3 57.6 us: paired_sums(): lax.psum(lax.psum((jnp.sum(residual * residual), jnp.sum(residual * image...]
    ppermute x6, starting transfers between devices: 15.6 us -> 11.8 us  [with_halo(): before = lax.ppermute(last, axis, up)]
where the time goes in v1:
time: 279 us; the launch traced here: 278 us
  waiting for transfers between devices  111 us (40%)
  blocking collectives  83.8 us (30%)
  other arithmetic  28.2 us (10%)
  between operations  23.5 us (8%)
  starting transfers between devices  19.5 us (7%)
  local copies, waits for them, and re-layouts  11.7 us (4%)
    psum x1, waiting for transfers between devices, local(): summed = lax.psum(partial_value, 'band')  86.5 us
    psum x3, blocking collectives, paired_sums(): lax.psum(lax.psum((jnp.sum(residual * residual), jnp.sum(residual * image...  57.6 us
    psum x3, blocking collectives, paired_sums(): lax.psum((jnp.sum(residual * residual), jnp.sum(residual * image)), 'space')  26.2 us
    ppermute x6, waiting for transfers between devices, with_halo(): after = lax.ppermute(first, axis, down)  23.4 us
    add x8, other arithmetic, accumulate(): return total + occupations[index] * wave * wave  20.1 us
    ppermute x6, starting transfers between devices, with_halo(): before = lax.ppermute(last, axis, up)  11.8 us
    dynamic_slice x8, local copies, waits for them, and re-layouts, accumulate(): return total + occupations[index] * wave * wave  10.6 us
    ppermute x6, starting transfers between devices, with_halo(): after = lax.ppermute(first, axis, down)  7.75 us
  transfers between devices with their start and end apart: 13, of which 10 were waited for; matrix products, arithmetic and copies ran while one was open for 0% of the time, Pallas kernels for 0%

profile of v1, /device:TPU:0, one launch (start us, length us, event | category | flops | bytes accessed | tf_op | source)
XLA Modules:
  0.0 277.8 jit_solution(15871623422627156158)
XLA Ops:
  6.5 30.8 %while.14 = (s32[]{:T(128)}, f32[64,40,128]{2,1,0:T(8,128)S(1)}, f32[8]{0:T(128)}, bf16[8,64,40,128]{3,2,1,0:T(8,128)(2,1)}, s32[]{:T(128)}, /*index=5*/s32[]{:T(128)}) while((s32[]{:T(128)}, f32[64,40,128]{2,1,0:T(8,128)S(1)}, f32[8]{0:T(128)}, bf16[8,64,40,128]{3,2,1,0:T(8,128)(2,1)}, s32[]{:T(128)}, /*index=5*/s32[]{:T(128)}) %tuple.46), condition=%wide.region_1.2_spmd.clone, body=%wide.region_0.1_spmd.clone.sunk | while | flops 1638403 | bytes 3276907 | solution.py:53
  6.5 1.3 dynamic_slice.31
  7.9 2.5 fusion.46
  10.4 1.3 dynamic_slice.31
  11.7 2.5 fusion.46
  14.2 1.3 dynamic_slice.31
  15.6 2.5 fusion.46
  18.1 1.3 dynamic_slice.31
  19.4 2.5 fusion.46
  21.9 1.3 dynamic_slice.31
  23.3 2.5 fusion.46
  25.8 1.3 dynamic_slice.31
  27.1 2.5 fusion.46
  29.6 1.3 dynamic_slice.31
  31.0 2.5 fusion.46
  33.5 1.3 dynamic_slice.31
  34.8 2.5 fusion.46
  37.3 1.1 copy-done
  38.4 86.5 %all-reduce.11.cloned.1.call-done = f32[64,40,128]{2,1,0:T(8,128)} async-done(((f32[64,40,128]{2,1,0:T(8,128)}), f32[64,40,128]{2,1,0:T(8,128)}) %all-reduce.11.cloned.1.call-update) | async-done | bytes 1310736 | tf_op jit(solution)/shard_map/psum | solution.py:55
  124.9 0.9 dynamic-slice_multiply_fusion
  125.9 3.4 %collective-permute-start.1 = (f32[2,40,128]{2,1,0:T(8,128)S(1)}, f32[2,40,128]{2,1,0:T(8,128)S(1)}, u32[]{:S(2)}, u32[]{:S(2)}) collective-permute-start(f32[2,40,128]{2,1,0:T(8,128)S(1)} %get-tuple-element.144), channel_id=1, source_target_pairs={{0,4},{4,8},{8,12},{12,16},{16,20},{20,24},{24,28},{1,5},{5,9},{9,... | collective-permute-start | bytes 122888 | tf_op jit(solution)/shard_map/ppermute | solution.py:18
  129.3 1.3 collective-permute-start
  130.9 4.2 %collective-permute-done = f32[2,40,128]{2,1,0:T(8,128)S(1)} collective-permute-done((f32[2,40,128]{2,1,0:T(8,128)S(1)}, f32[2,40,128]{2,1,0:T(8,128)S(1)}, u32[]{:S(2)}, u32[]{:S(2)}) %collective-permute-start) | collective-permute-done | bytes 40992 | tf_op jit(solution)/shard_map/ppermute | solution.py:19
  135.2 1.3 collective-permute-start.3
  136.5 1.3 collective-permute-start.2
  137.8 3.5 %collective-permute-done.2 = f32[12,2,128]{2,1,0:T(2,128)S(1)} collective-permute-done((f32[12,2,128]{2,1,0:T(2,128)S(1)}, f32[12,2,128]{2,1,0:T(2,128)S(1)}, u32[]{:S(2)}, u32[]{:S(2)}) %collective-permute-start.2) | collective-permute-done | bytes 12320 | tf_op jit(solution)/shard_map/ppermute | solution.py:19
  141.6 1.8 multiply_reduce_fusion.3
  143.4 8.7 %all-reduce.8 = (f32[]{:T(128)}, f32[]{:T(128)}) all-reduce(f32[]{:T(128)} %get-tuple-element.105, f32[]{:T(128)} %get-tuple-element.104), channel_id=1, replica_groups=mesh['band'=8,'space'=4] {'space'}, use_global_device_ids=true, to_apply=%region_4.5 | all-reduce | flops 2 | bytes 16 | tf_op jit(solution)/shard_map/psum | solution.py:42
  152.1 19.9 %all-reduce.5 = (f32[]{:T(128)}, f32[]{:T(128)}) all-reduce(f32[]{:T(128)} %get-tuple-element.124, f32[]{:T(128)} %get-tuple-element.125), channel_id=1, replica_groups=mesh['band'=8,'space'=4] {'band'}, use_global_device_ids=true, to_apply=%region_5.6 | all-reduce | flops 2 | bytes 16 | tf_op jit(solution)/shard_map/psum | solution.py:41
  173.3 0.9 multiply_subtract_fusion.1
  174.2 1.8 collective-permute-start.5
  176.1 1.3 collective-permute-start.4
  177.7 4.2 %collective-permute-done.4 = f32[2,40,128]{2,1,0:T(8,128)S(1)} collective-permute-done((f32[2,40,128]{2,1,0:T(8,128)S(1)}, f32[2,40,128]{2,1,0:T(8,128)S(1)}, u32[]{:S(2)}, u32[]{:S(2)}) %collective-permute-start.4) | collective-permute-done | bytes 40992 | tf_op jit(solution)/shard_map/ppermute | solution.py:19
  182.0 1.3 collective-permute-start.7
  183.3 1.3 collective-permute-start.6
  184.6 3.6 %collective-permute-done.6 = f32[12,2,128]{2,1,0:T(2,128)S(1)} collective-permute-done((f32[12,2,128]{2,1,0:T(2,128)S(1)}, f32[12,2,128]{2,1,0:T(2,128)S(1)}, u32[]{:S(2)}, u32[]{:S(2)}) %collective-permute-start.6) | collective-permute-done | bytes 12320 | tf_op jit(solution)/shard_map/ppermute | solution.py:19
  189.4 8.8 %all-reduce.7 = (f32[]{:T(128)}, f32[]{:T(128)}) all-reduce(f32[]{:T(128)} %get-tuple-element.103, f32[]{:T(128)} %get-tuple-element.102), channel_id=1, replica_groups=mesh['band'=8,'space'=4] {'space'}, use_global_device_ids=true, to_apply=%region_10.11 | all-reduce | flops 2 | bytes 16 | tf_op jit(solution)/shard_map/psum | solution.py:42
  198.2 19.0 %all-reduce.4 = (f32[]{:T(128)}, f32[]{:T(128)}) all-reduce(f32[]{:T(128)} %get-tuple-element.122, f32[]{:T(128)} %get-tuple-element.123), channel_id=1, replica_groups=mesh['band'=8,'space'=4] {'band'}, use_global_device_ids=true, to_apply=%region_11.12 | all-reduce | flops 2 | bytes 16 | tf_op jit(solution)/shard_map/psum | solution.py:41
  221.7 2.7 collective-permute-start.9
  224.5 1.3 collective-permute-start.8
  226.1 4.2 %collective-permute-done.8 = f32[2,40,128]{2,1,0:T(8,128)S(1)} collective-permute-done((f32[2,40,128]{2,1,0:T(8,128)S(1)}, f32[2,40,128]{2,1,0:T(8,128)S(1)}, u32[]{:S(2)}, u32[]{:S(2)}) %collective-permute-start.8) | collective-permute-done | bytes 40992 | tf_op jit(solution)/shard_map/ppermute | solution.py:19
  230.4 1.3 collective-permute-start.11
  231.7 1.3 collective-permute-start.10
  233.0 3.6 %collective-permute-done.10 = f32[12,2,128]{2,1,0:T(2,128)S(1)} collective-permute-done((f32[12,2,128]{2,1,0:T(2,128)S(1)}, f32[12,2,128]{2,1,0:T(2,128)S(1)}, u32[]{:S(2)}, u32[]{:S(2)}) %collective-permute-start.10) | collective-permute-done | bytes 12320 | tf_op jit(solution)/shard_map/ppermute | solution.py:19
  236.9 0.9 fusion.39
  237.9 8.7 %all-reduce.6 = (f32[]{:T(128)}, f32[]{:T(128)}) all-reduce(f32[]{:T(128)} %get-tuple-element.101, f32[]{:T(128)} %get-tuple-element.100), channel_id=1, replica_groups=mesh['band'=8,'space'=4] {'space'}, use_global_device_ids=true, to_apply=%region_16.17 | all-reduce | flops 2 | bytes 16 | tf_op jit(solution)/shard_map/psum | solution.py:42
  246.6 18.7 %all-reduce.3 = (f32[]{:T(128)}, f32[]{:T(128)}) all-reduce(f32[]{:T(128)} %get-tuple-element.120, f32[]{:T(128)} %get-tuple-element.121), channel_id=1, replica_groups=mesh['band'=8,'space'=4] {'band'}, use_global_device_ids=true, to_apply=%region_17.18 | all-reduce | flops 2 | bytes 16 | tf_op jit(solution)/shard_map/psum | solution.py:41
  269.3 1.6 multiply_add_fusion
  (24 shorter events, 3.0 us)
Async XLA Ops:
  6.5 118.4 %all-reduce.11.cloned.1.call-start = ((), (), s32[]{:S(2)}) async-start(), calls=%async_computation | async-start | bytes 2621440 | tf_op jit(solution)/shard_map/psum | solution.py:55
  37.3 1.1 copy-start
  125.9 5.0 %collective-permute-start.1 = (f32[2,40,128]{2,1,0:T(8,128)S(1)}, f32[2,40,128]{2,1,0:T(8,128)S(1)}, u32[]{:S(2)}, u32[]{:S(2)}) collective-permute-start(f32[2,40,128]{2,1,0:T(8,128)S(1)} %get-tuple-element.144), channel_id=1, source_target_pairs={{0,4},{4,8},{8,12},{12,16},{16,20},{20,24},{24,28},{1,5},{5,9},{9,... | collective-permute-start | bytes 122888 | tf_op jit(solution)/shard_map/ppermute | solution.py:18
  129.3 5.9 %collective-permute-start = (f32[2,40,128]{2,1,0:T(8,128)S(1)}, f32[2,40,128]{2,1,0:T(8,128)S(1)}, u32[]{:S(2)}, u32[]{:S(2)}) collective-permute-start(f32[2,40,128]{2,1,0:T(8,128)S(1)} %get-tuple-element.145), channel_id=1, source_target_pairs={{4,0},{8,4},{12,8},{16,12},{20,16},{24,20},{28,24},{5,1},{9,5},{13... | collective-permute-start | bytes 122888 | tf_op jit(solution)/shard_map/ppermute | solution.py:19
  135.2 2.6 collective-permute-start.3
  136.5 4.8 %collective-permute-start.2 = (f32[12,2,128]{2,1,0:T(2,128)S(1)}, f32[12,2,128]{2,1,0:T(2,128)S(1)}, u32[]{:S(2)}, u32[]{:S(2)}) collective-permute-start(f32[12,2,128]{2,1,0:T(2,128)S(1)} %get-tuple-element.139), channel_id=1, source_target_pairs={{1,0},{2,1},{3,2},{5,4},{6,5},{7,6},{9,8},{10,9},{11,10},{13,12},{... | collective-permute-start | bytes 36872 | tf_op jit(solution)/shard_map/ppermute | solution.py:19
  174.2 3.5 %collective-permute-start.5 = (f32[2,40,128]{2,1,0:T(8,128)S(1)}, f32[2,40,128]{2,1,0:T(8,128)S(1)}, u32[]{:S(2)}, u32[]{:S(2)}) collective-permute-start(f32[2,40,128]{2,1,0:T(8,128)S(1)} %get-tuple-element.142), channel_id=1, source_target_pairs={{0,4},{4,8},{8,12},{12,16},{16,20},{20,24},{24,28},{1,5},{5,9},{9,... | collective-permute-start | bytes 122888 | tf_op jit(solution)/shard_map/ppermute | solution.py:18
  176.1 5.9 %collective-permute-start.4 = (f32[2,40,128]{2,1,0:T(8,128)S(1)}, f32[2,40,128]{2,1,0:T(8,128)S(1)}, u32[]{:S(2)}, u32[]{:S(2)}) collective-permute-start(f32[2,40,128]{2,1,0:T(8,128)S(1)} %get-tuple-element.143), channel_id=1, source_target_pairs={{4,0},{8,4},{12,8},{16,12},{20,16},{24,20},{28,24},{5,1},{9,5},{13... | collective-permute-start | bytes 122888 | tf_op jit(solution)/shard_map/ppermute | solution.py:19
  182.0 2.6 collective-permute-start.7
  183.3 4.9 %collective-permute-start.6 = (f32[12,2,128]{2,1,0:T(2,128)S(1)}, f32[12,2,128]{2,1,0:T(2,128)S(1)}, u32[]{:S(2)}, u32[]{:S(2)}) collective-permute-start(f32[12,2,128]{2,1,0:T(2,128)S(1)} %get-tuple-element.135), channel_id=1, source_target_pairs={{1,0},{2,1},{3,2},{5,4},{6,5},{7,6},{9,8},{10,9},{11,10},{13,12},{... | collective-permute-start | bytes 36872 | tf_op jit(solution)/shard_map/ppermute | solution.py:19
  221.7 4.4 %collective-permute-start.9 = (f32[2,40,128]{2,1,0:T(8,128)S(1)}, f32[2,40,128]{2,1,0:T(8,128)S(1)}, u32[]{:S(2)}, u32[]{:S(2)}) collective-permute-start(f32[2,40,128]{2,1,0:T(8,128)S(1)} %get-tuple-element.140), channel_id=1, source_target_pairs={{0,4},{4,8},{8,12},{12,16},{16,20},{20,24},{24,28},{1,5},{5,9},{9,... | collective-permute-start | bytes 122888 | tf_op jit(solution)/shard_map/ppermute | solution.py:18
  224.5 5.9 %collective-permute-start.8 = (f32[2,40,128]{2,1,0:T(8,128)S(1)}, f32[2,40,128]{2,1,0:T(8,128)S(1)}, u32[]{:S(2)}, u32[]{:S(2)}) collective-permute-start(f32[2,40,128]{2,1,0:T(8,128)S(1)} %get-tuple-element.141), channel_id=1, source_target_pairs={{4,0},{8,4},{12,8},{16,12},{20,16},{24,20},{28,24},{5,1},{9,5},{13... | collective-permute-start | bytes 122888 | tf_op jit(solution)/shard_map/ppermute | solution.py:19
  230.4 2.6 collective-permute-start.11
  231.7 4.9 %collective-permute-start.10 = (f32[12,2,128]{2,1,0:T(2,128)S(1)}, f32[12,2,128]{2,1,0:T(2,128)S(1)}, u32[]{:S(2)}, u32[]{:S(2)}) collective-permute-start(f32[12,2,128]{2,1,0:T(2,128)S(1)} %get-tuple-element.131), channel_id=1, source_target_pairs={{1,0},{2,1},{3,2},{5,4},{6,5},{7,6},{9,8},{10,9},{11,10},{13,12},{... | collective-permute-start | bytes 36872 | tf_op jit(solution)/shard_map/ppermute | solution.py:19
Sparse Core Ops, SparseCore 0:
  38.6 86.3 all-reduce.10
